TPU v7x, 32 devices: a whole 2x2x4 slice. The times are simulated.
32 devices in a mesh: dp: 8 (over z, x), expert: 4 (over y, core).
Axes of the slice: x: 2, y: 2, z: 4, core: 2. Of those that a mesh axis runs over, the one named last changes fastest.
Arguments:
- tokens: bfloat16 [4096, 4096], P(('dp', 'expert')), may hold values from -6 to 6
- select: int32 [4, 128], P(None, ('dp', 'expert')), may hold values from -1 to 127, as said below
- gates: float32 [4, 128], P(None, ('dp', 'expert')), may hold values from 0.1 to 1
- w_gate: bfloat16 [4, 4096, 8192], P('expert', None, 'dp'), may hold values from -0.09375 to 0.09375
- w_up: bfloat16 [4, 4096, 8192], P('expert', None, 'dp'), may hold values from -0.09375 to 0.09375
- w_down: bfloat16 [4, 8192, 4096], P('expert', 'dp'), may hold values from -0.0625 to 0.0625
Outputs:
- mixed: bfloat16 [4096, 4096], P(('dp', 'expert'))
Inputs may be any that keep to these rules, and one draw needn't show every extreme that they name: `select`: in each block of 4 slots of a row, the live entries come first, distinct and ascending, below 128, followed by -1; every block holds at least one live entry, and every expert fills all 4 slots of some source device.
All inputs are finite; a program needn't handle non-finite values.
Results may differ from a plain program's by a relative error of at most 0.0085.
Values may be sent and summed in bfloat16 or wider, within the bound.
A program may use at most 64 MiB of HBM per device.

v0:
```python
import jax
import jax.numpy as jnp
from jax import lax
from jax.sharding import PartitionSpec as P


def expert_ffn(block_rows, w_gate, w_up, w_down):
    gate_val = jnp.einsum("erd,edf->erf", block_rows, w_gate, preferred_element_type=jnp.float32)
    up_val = jnp.einsum("erd,edf->erf", block_rows, w_up, preferred_element_type=jnp.float32)
    hidden = (jax.nn.silu(gate_val) * up_val).astype(jnp.bfloat16)
    return jnp.einsum("erf,efd->erd", hidden, w_down, preferred_element_type=jnp.float32)


def per_device(tokens, select, gates, w_gate, w_up, w_down):
    experts, slot_count = select.shape
    tok_dev, width = tokens.shape
    is_live = select >= 0
    safe_idx = jnp.where(is_live, select, 0)
    sel_rows = jnp.take(tokens, safe_idx.reshape(-1), axis=0).reshape(experts, slot_count, width)
    sel_rows = jnp.where(is_live[:, :, None], sel_rows, 0)
    arrived = lax.all_to_all(sel_rows, "expert", split_axis=0, concat_axis=1, tiled=True)
    partial_value = expert_ffn(
        lax.all_gather(arrived, "dp", axis=1, tiled=True), w_gate, w_up, w_down
    )
    summed = lax.psum_scatter(partial_value, "dp", scatter_dimension=1, tiled=True)
    returned = lax.all_to_all(
        summed.astype(jnp.bfloat16), "expert", split_axis=1, concat_axis=0, tiled=True
    )
    weight_flat = jnp.where(is_live, gates, 0.0).reshape(-1)
    token_ids = jnp.arange(tok_dev, dtype=jnp.int32)
    combine = jnp.where(
        safe_idx.reshape(-1)[None, :] == token_ids[:, None], weight_flat[None, :], 0.0
    )
    mixed = jnp.dot(
        combine, returned.reshape(-1, width).astype(jnp.float32), precision=lax.Precision.HIGHEST
    )
    return mixed.astype(jnp.bfloat16)


def solution(mesh):
    return jax.shard_map(
        per_device,
        mesh=mesh,
        in_specs=(
            P(("dp", "expert"), None),
            P(None, ("dp", "expert")),
            P(None, ("dp", "expert")),
            P("expert", None, "dp"),
            P("expert", None, "dp"),
            P("expert", "dp", None),
        ),
        out_specs=P(("dp", "expert"), None),
        check_vma=False,
    )
```

profile of v0, /device:TPU:0, one launch (start us, length us, event | category | flops | bytes accessed | tf_op | source)
XLA Modules:
  0.0 161.7 jit_solution(17055922872757218782)
XLA Ops:
  6.5 0.0 copy-start
  6.5 0.0 all-gather.2.cloned.1.call-start
  6.5 0.8 broadcast_select_fusion
  7.3 0.7 compare_and_fusion
  8.0 0.1 reshape.81
  8.1 0.0 copy-done
  8.1 0.6 gather_fusion
  8.8 0.1 gather.7
  8.8 0.1 select_select_fusion
  9.0 8.7 %all_to_all.21 = bf16[4,4,4096]{2,1,0:T(4,128)(2,1)S(1)} all-to-all(bf16[4,4,4096]{2,1,0:T(4,128)(2,1)S(1)} %select_select_fusion), channel_id=1, replica_groups=mesh['dp'=8,'expert'=4] {'expert'}, dimensions={0} | all-to-all | bytes 262144 | tf_op jit(solution)/shard_map/all_to_all | solution.py:21
  17.6 0.7 all_to_all.7
  18.3 0.0 all-gather.2.cloned.1.call-update
  18.3 0.0 reduce-scatter.2.cloned.1.call-start
  18.4 40.7 %all-gather.2.cloned.1.call-done = bf16[1,128,4096]{2,1,0:T(8,128)(2,1)} async-done(((bf16[1,16,4096]{2,1,0:T(8,128)(2,1)}), bf16[1,128,4096]{2,1,0:T(8,128)(2,1)}) %all-gather.2.cloned.1.call-update) | async-done | bytes 1048592 | tf_op jit(solution)/shard_map/all_gather | solution.py:23
  59.1 0.0 copy-start.1
  59.1 5.0 %fusion.4 = f32[128,1024]{1,0:T(8,128)S(1)} fusion(bf16[1,4096,1024]{2,1,0:T(8,128)(2,1)} %param.9, bf16[1,128,4096]{2,1,0:T(8,128)(2,1)} %all-gather.2.cloned.1.call-done), kind=kOutput, calls=%fused_computation.5 | convolution fusion | flops 1073741824 | bytes 9961472 | tf_op jit(solution)/shard_map/erd,edf->erf/dot_general | solution.py:8
  64.1 0.0 copy-done.1
  64.1 9.6 %fusion.6 = f32[1,128,4096]{2,1,0:T(8,128)} fusion(bf16[1,1024,4096]{2,1,0:T(8,128)(2,1)} %param.11, bf16[1,4096,1024]{2,1,0:T(8,128)(2,1)} %param.10, bf16[1,128,4096]{2,1,0:T(8,128)(2,1)S(1)} %copy-done.1, f32[128,1024]{1,0:T(8,128)S(1)} %fusion.4), kind=kOutput, calls=%fused_computation.7 | convolution fusion | flops 2148270080 | bytes 20447232 | tf_op jit(solution)/shard_map/erf,efd->erd/dot_general | solution.py:11
  73.7 0.0 reduce-scatter.2.cloned.1.call-update
  73.7 67.3 %reduce-scatter.2.cloned.1.call-done = f32[1,16,4096]{2,1,0:T(8,128)} async-done(((f32[1,128,4096]{2,1,0:T(8,128)}), f32[1,16,4096]{2,1,0:T(8,128)}) %reduce-scatter.2.cloned.1.call-update) | async-done | bytes 262160 | tf_op jit(solution)/shard_map/reduce_scatter | solution.py:25
  141.0 1.0 convert_element_type.14
  142.0 0.2 copy.15
  142.2 0.5 broadcast.57
  142.7 1.4 reduce
  144.1 0.8 reshape.95
  144.9 3.3 %all-to-all-start.1 = ((bf16[4,2,8192]{2,1,0:T(2,128)(2,1)}), bf16[4,2,8192]{2,1,0:T(2,128)(2,1)S(1)}, u32[]{:S(2)}, u32[]{:S(2)}) async-start(bf16[4,2,8192]{2,1,0:T(2,128)(2,1)} %reshape.95), calls=%async_computation.2 | async-start | bytes 262144 | tf_op jit(solution)/shard_map/all_to_all | solution.py:26
  148.2 0.1 eq.15
  148.3 0.1 broadcast_in_dim.45
  148.4 4.4 %all-to-all-done.1 = bf16[4,2,8192]{2,1,0:T(2,128)(2,1)S(1)} async-done(((bf16[4,2,8192]{2,1,0:T(2,128)(2,1)}), bf16[4,2,8192]{2,1,0:T(2,128)(2,1)S(1)}, u32[]{:S(2)}, u32[]{:S(2)}) %all-to-all-start.1) | async-done | bytes 131104 | tf_op jit(solution)/shard_map/all_to_all | solution.py:26
  152.8 0.1 reshape.96
  152.9 2.0 %convolution_convert_fusion = bf16[128,4096]{1,0:T(8,128)(2,1)} fusion(bf16[1,16,4096]{2,0,1:T(2,128)(2,1)S(1)} %bitcast.36, f32[16]{0:T(128)S(1)} %broadcast_in_dim.45, s32[16]{0:T(128)S(1)} %eq.15), kind=kOutput, calls=%fused_computation.8 | convolution fusion | flops 101191680 | bytes 1179776 | tf_op jit(solution)/shard_map/dot_general | solution.py:34
  (2 shorter events, 0.0 us)
Async XLA Ops:
  6.5 1.6 copy-start
  6.5 52.5 %all-gather.2.cloned.1.call-start = ((), (), s32[]{:S(2)}) async-start(), calls=%async_computation.3 | async-start | bytes 1179648 | tf_op jit(solution)/shard_map/all_gather | solution.py:23
  18.3 122.7 %reduce-scatter.2.cloned.1.call-start = ((), (), s32[]{:S(2)}) async-start(), calls=%async_computation.4 | async-start | bytes 2359296 | tf_op jit(solution)/shard_map/reduce_scatter | solution.py:25
  59.1 5.0 %copy-start.1 = (bf16[1,128,4096]{2,1,0:T(8,128)(2,1)S(1)}, bf16[1,128,4096]{2,1,0:T(8,128)(2,1)}, u32[]{:S(2)}) copy-start(bf16[1,128,4096]{2,1,0:T(8,128)(2,1)} %all-gather.2.cloned.1.call-done) | copy-start | bytes 3145732
  144.9 7.9 %all-to-all-start.1 = ((bf16[4,2,8192]{2,1,0:T(2,128)(2,1)}), bf16[4,2,8192]{2,1,0:T(2,128)(2,1)S(1)}, u32[]{:S(2)}, u32[]{:S(2)}) async-start(bf16[4,2,8192]{2,1,0:T(2,128)(2,1)} %reshape.95), calls=%async_computation.2 | async-start | bytes 262144 | tf_op jit(solution)/shard_map/all_to_all | solution.py:26
Sparse Core Ops, SparseCore 0:
  18.5 40.5 all-gather.1
  73.8 67.1 reduce-scatter.1
where the time goes:
time: 162 us
  waiting for transfers between devices  112 us (69%)
  matrix products  16.6 us (10%)
  between operations  13.5 us (8%)
  blocking collectives  8.67 us (5%)
  other arithmetic  3.97 us (2%)
  starting transfers between devices  3.37 us (2%)
  local copies, waits for them, and re-layouts  3.28 us (2%)
    reduce_scatter x1, waiting for transfers between devices, per_device(): lax.psum_scatter(partial_value, 'dp', scatter_dimension=1, tiled=True)  67.3 us
    all_gather x1, waiting for transfers between devices, per_device(): lax.all_gather(arrived, 'dp', axis=1, tiled=True)  40.7 us
    dot_general x1, matrix products, expert_ffn(): jnp.einsum('erf,efd->erd', hidden, w_down, preferred_element_type=jnp.flo...  9.57 us
    all_to_all x1, blocking collectives, per_device(): lax.all_to_all(sel_rows, 'expert', split_axis=0, concat_axis=1, tiled=True)  8.67 us
    dot_general x1, matrix products, expert_ffn(): jnp.einsum('erd,edf->erf', block_rows, w_gate, preferred_element_type=jnp...  5.03 us
    all_to_all x1, waiting for transfers between devices, per_device(): lax.all_to_all(summed.astype(jnp.bfloat16), 'expert', split_axis=1, conca...  4.4 us
    all_to_all x1, starting transfers between devices, per_device(): lax.all_to_all(summed.astype(jnp.bfloat16), 'expert', split_axis=1, conca...  3.33 us
  transfers between devices with their start and end apart: 3, of which 3 were waited for; matrix products, arithmetic and copies ran while one was open for 0% of the time, Pallas kernels for 0%

commit v1 on v0

v1 whole, which is shorter than its diff:
```python
import functools

import jax
import jax.numpy as jnp
from jax import lax
from jax.experimental import pallas as pl
from jax.experimental.pallas import tpu as pltpu
from jax.sharding import PartitionSpec as P

MESH = pl.DeviceIdType.MESH
TILE = 16
F32 = jnp.float32
BF16 = jnp.bfloat16


def log2(n):
    return n.bit_length() - 1


def kernel(
    nd, ne, tok, sel, gat, wg_hbm, wu_hbm, wd_hbm, out,
    wg, wu, wd, sb, ab, x, hid, pb, xr, zb, zr, summed, rb, ob, cmb,
    w_sem, a_send, a_recv, gz_send, gz_recv, gx_send, gx_recv,
    rx_send, rx_recv, rz_send, rz_recv, o_send, o_recv,
):
    inner = x.shape[0]
    outer = x.shape[1]
    rows = x.shape[2]
    slots = sel.shape[1]
    tokens_here = tok.shape[0]
    parts = TILE // slots
    wide = sb.shape[2]
    chunks = pb.shape[0]
    cols = pb.shape[4]
    dp = lax.axis_index("dp")
    ex = lax.axis_index("expert")
    za = dp // inner
    xb = lax.rem(dp, inner)
    other = (inner - 1) - xb

    def at_expert(d):
        return (dp, lax.rem(ex + d, ne))

    def at_outer(d):
        return (lax.rem(za + d, outer) * inner + xb, ex)

    partner = (za * inner + other, ex)

    def remote(src, dst, send, recv, to):
        return pltpu.make_async_remote_copy(
            src_ref=src, dst_ref=dst, send_sem=send, recv_sem=recv,
            device_id=to, device_id_type=MESH,
        )

    barrier = pltpu.get_barrier_semaphore()
    for d in range(1, ne):
        pl.semaphore_signal(barrier, inc=1, device_id=at_expert(d), device_id_type=MESH)
    for d in range(1, outer):
        pl.semaphore_signal(barrier, inc=1, device_id=at_outer(d), device_id_type=MESH)
    if inner > 1:
        pl.semaphore_signal(barrier, inc=1, device_id=partner, device_id_type=MESH)

    loads = [
        pltpu.make_async_copy(h.at[0], v, w_sem.at[i])
        for i, (h, v) in enumerate(((wg_hbm, wg), (wu_hbm, wu), (wd_hbm, wd)))
    ]
    for load in loads:
        load.start()

    packed = ne * TILE
    r_id = lax.broadcasted_iota(jnp.int32, (packed, tokens_here), 0)
    t_id = lax.broadcasted_iota(jnp.int32, (packed, tokens_here), 1)
    r_slot = ((r_id >> log2(TILE)) << log2(slots)) + (r_id & (slots - 1))
    r_part = (r_id & (TILE - 1)) >> log2(slots)
    named = jnp.full((packed, tokens_here), -1, jnp.int32)
    for e in range(ne):
        for s in range(slots):
            named = jnp.where(r_slot == e * slots + s, sel[e, s], named)
    hit = jnp.where(named == t_id, 1.0, 0.0)
    pick = jnp.concatenate(
        [jnp.where(r_part == q, hit, 0.0).astype(BF16) for q in range(parts)], axis=1
    )
    stack = jnp.concatenate([tok[:, q * wide:(q + 1) * wide] for q in range(parts)], axis=0)
    gathered = jnp.dot(pick, stack, preferred_element_type=F32).astype(BF16)
    sb[...] = gathered.reshape(ne, TILE, wide)
    ab[ex] = sb[ex]

    pl.semaphore_wait(barrier, (ne - 1) + (outer - 1) + (1 if inner > 1 else 0))

    a_copies = []
    for d in range(1, ne):
        to = at_expert(d)
        copy = remote(sb.at[to[1]], ab.at[ex], a_send.at[d], a_recv.at[d], to)
        copy.start()
        a_copies.append(copy)

    c_id = lax.broadcasted_iota(jnp.int32, (tokens_here, packed), 1)
    n_id = lax.broadcasted_iota(jnp.int32, (tokens_here, packed), 0)
    c_slot = ((c_id >> log2(TILE)) << log2(slots)) + (c_id & (slots - 1))
    weight = jnp.zeros((tokens_here, packed), F32)
    for e in range(ne):
        for s in range(slots):
            weight = jnp.where((c_slot == e * slots + s) & (n_id == sel[e, s]), gat[e, s], weight)
    left = weight
    for i in range(3):
        term = left.astype(BF16)
        cmb[i] = term
        left = left - term.astype(F32)

    u_r = lax.broadcasted_iota(jnp.int32, (packed, parts * rows), 0)
    u_k = lax.broadcasted_iota(jnp.int32, (packed, parts * rows), 1)
    u_col = (
        ((u_r & (TILE - 1)) >> log2(slots)) * rows
        + ((u_r >> log2(TILE)) << log2(slots)) + (u_r & (slots - 1))
    )
    pack = jnp.where(u_k == u_col, 1.0, 0.0).astype(BF16)
    v_r = lax.broadcasted_iota(jnp.int32, (parts * rows, packed), 0)
    v_k = lax.broadcasted_iota(jnp.int32, (parts * rows, packed), 1)
    v_row = (
        ((v_k & (TILE - 1)) >> log2(slots)) * rows
        + ((v_k >> log2(TILE)) << log2(slots)) + (v_k & (slots - 1))
    )
    unpack = jnp.where(v_r == v_row, 1.0, 0.0).astype(BF16)

    for d in range(1, ne):
        src = lax.rem(ex + ne - d, ne)
        remote(sb.at[src], ab.at[src], a_send.at[d], a_recv.at[d], at_expert(d)).wait_recv()
    mine = jnp.dot(unpack, ab[...].reshape(packed, wide), preferred_element_type=F32).astype(BF16)
    for q in range(parts):
        x[xb, za, :, q * wide:(q + 1) * wide] = mine[q * rows:(q + 1) * rows]

    own = x.at[xb, za]
    z_copies = []
    for d in range(1, outer):
        copy = remote(own, own, gz_send.at[d], gz_recv.at[d], at_outer(d))
        copy.start()
        z_copies.append(copy)
    x_copies = []

    def forward(d):
        block = x.at[xb, lax.rem(za + outer - d, outer)]
        copy = remote(block, block, gx_send.at[d], gx_recv.at[d], partner)
        copy.start()
        x_copies.append(copy)

    order = sorted(range(1, outer), key=lambda d: (min(d, outer - d), d))
    if inner > 1:
        forward(0)
    for d in order:
        block = x.at[xb, lax.rem(za + outer - d, outer)]
        remote(block, block, gz_send.at[d], gz_recv.at[d], at_outer(d)).wait_recv()
        if inner > 1:
            forward(d)
    if inner > 1:
        for d in [0] + order:
            block = x.at[other, lax.rem(za + outer - d, outer)]
            remote(block, block, gx_send.at[d], gx_recv.at[d], partner).wait_recv()

    loads[0].wait()
    loads[1].wait()
    total_rows = inner * outer * rows
    step = min(256, hid.shape[1])

    @pl.loop(0, hid.shape[1] // step)
    def _(i):
        at = pl.ds(pl.multiple_of(i * step, step), step)
        block = x[...].reshape(total_rows, x.shape[3])
        g = jnp.dot(block, wg[:, at], preferred_element_type=F32)
        u = jnp.dot(block, wu[:, at], preferred_element_type=F32)
        hid[:, at] = (g / (1.0 + jnp.exp(-g)) * u).astype(BF16)

    loads[2].wait()

    def rx(c):
        return remote(pb.at[c, other], xr.at[c], rx_send.at[c], rx_recv.at[c], partner)

    @pl.loop(0, chunks)
    def _(c):
        at = pl.ds(pl.multiple_of(c * cols, cols), cols)
        part = jnp.dot(hid[...], wd[:, at], preferred_element_type=F32)
        pb[c] = part.astype(BF16).reshape(inner, outer, rows, cols)
        if inner > 1:
            rx(c).start()

    def rz(c, d):
        to = lax.rem(za + d, outer)
        return remote(zb.at[c, to], zr.at[c, d - 1], rz_send.at[c, d], rz_recv.at[c, d], at_outer(d))

    @pl.loop(0, chunks)
    def _(c):
        value = pb[c, xb].astype(F32)
        if inner > 1:
            rx(c).wait_recv()
            value = value + xr[c].astype(F32)
        zb[c] = value.astype(BF16)
        for d in range(1, outer):
            rz(c, d).start()

    per = wide // cols
    for c in range(chunks):
        value = zb[c, za].astype(F32)
        for d in range(1, outer):
            rz(c, d).wait_recv()
            value = value + zr[c, d - 1].astype(F32)
        at = (c % per) * cols
        summed[c // per, :, at:at + cols] = value.astype(BF16)

    back = jnp.dot(pack, summed[...].reshape(parts * rows, wide), preferred_element_type=F32)
    rb[...] = back.astype(BF16).reshape(ne, TILE, wide)
    ob[ex] = rb[ex]
    o_copies = []
    for d in range(1, ne):
        to = at_expert(d)
        copy = remote(rb.at[to[1]], ob.at[ex], o_send.at[d], o_recv.at[d], to)
        copy.start()
        o_copies.append(copy)
    for d in range(1, ne):
        src = lax.rem(ex + ne - d, ne)
        remote(rb.at[src], ob.at[src], o_send.at[d], o_recv.at[d], at_expert(d)).wait_recv()
    got = ob[...].reshape(packed, wide)
    c_part = (c_id & (TILE - 1)) >> log2(slots)
    for q in range(parts):
        total = jnp.zeros((tokens_here, wide), F32)
        for i in range(2, -1, -1):
            coef = jnp.where(c_part == q, cmb[i].astype(F32), 0.0).astype(BF16)
            total = total + jnp.dot(coef, got, preferred_element_type=F32)
        out[:, q * wide:(q + 1) * wide] = total.astype(BF16)

    for copy in a_copies + z_copies + x_copies + o_copies:
        copy.wait_send()

    @pl.loop(0, chunks)
    def _(c):
        if inner > 1:
            rx(c).wait_send()
        for d in range(1, outer):
            rz(c, d).wait_send()


def per_device(nd, ne, tokens, select, gates, w_gate, w_up, w_down):
    tok_dev, width = tokens.shape
    slots = select.shape[1]
    hidden = w_gate.shape[2]
    inner = 2 if nd % 2 == 0 else 1
    outer = nd // inner
    rows = ne * slots
    wide = width * slots // TILE
    parts = TILE // slots
    cols = min(512, wide)
    chunks = width // cols
    vmem = pl.BlockSpec(memory_space=pltpu.VMEM)
    smem = pl.BlockSpec(memory_space=pltpu.SMEM)
    hbm = pl.BlockSpec(memory_space=pl.ANY)
    dma = pltpu.SemaphoreType.DMA
    return pl.pallas_call(
        functools.partial(kernel, nd, ne),
        out_shape=jax.ShapeDtypeStruct((tok_dev, width), BF16),
        in_specs=[vmem, smem, smem, hbm, hbm, hbm],
        out_specs=vmem,
        scratch_shapes=[
            pltpu.VMEM((width, hidden), BF16),
            pltpu.VMEM((width, hidden), BF16),
            pltpu.VMEM((hidden, width), BF16),
            pltpu.VMEM((ne, TILE, wide), BF16),
            pltpu.VMEM((ne, TILE, wide), BF16),
            pltpu.VMEM((inner, outer, rows, width), BF16),
            pltpu.VMEM((nd * rows, hidden), BF16),
            pltpu.VMEM((chunks, inner, outer, rows, cols), BF16),
            pltpu.VMEM((chunks, outer, rows, cols), BF16),
            pltpu.VMEM((chunks, outer, rows, cols), BF16),
            pltpu.VMEM((chunks, max(outer - 1, 1), rows, cols), BF16),
            pltpu.VMEM((parts, rows, wide), BF16),
            pltpu.VMEM((ne, TILE, wide), BF16),
            pltpu.VMEM((ne, TILE, wide), BF16),
            pltpu.VMEM((3, tok_dev, ne * TILE), BF16),
            dma((3,)),
            dma((ne,)), dma((ne,)),
            dma((outer,)), dma((outer,)),
            dma((outer,)), dma((outer,)),
            dma((chunks,)), dma((chunks,)),
            dma((chunks, outer)), dma((chunks, outer)),
            dma((ne,)), dma((ne,)),
        ],
        compiler_params=pltpu.CompilerParams(
            collective_id=0, has_side_effects=True, vmem_limit_bytes=60 * 1024 * 1024
        ),
    )(tokens, select, gates, w_gate, w_up, w_down)


def solution(mesh):
    return jax.shard_map(
        functools.partial(per_device, mesh.shape["dp"], mesh.shape["expert"]),
        mesh=mesh,
        in_specs=(
            P(("dp", "expert"), None),
            P(None, ("dp", "expert")),
            P(None, ("dp", "expert")),
            P("expert", None, "dp"),
            P("expert", None, "dp"),
            P("expert", "dp", None),
        ),
        out_specs=P(("dp", "expert"), None),
        check_vma=False,
    )
```

time: 162 us -> 56.1 us (0.35)
  waiting for transfers between devices: 112 us -> 0 us
  Pallas kernels: 0 us -> 53.7 us
  matrix products: 16.6 us -> 0 us
  between operations: 13.5 us -> 0.01 us
  blocking collectives: 8.67 us -> 0 us
  other arithmetic: 3.97 us -> 0 us
  starting transfers between devices: 3.37 us -> 0 us
    reduce_scatter x1 -> x0, waiting for transfers between devices: 67.3 us -> none  [per_device(): lax.psum_scatter(partial_value, 'dp', scatter_dimension=1, tiled=True)]
    pallas_call x0 -> x1, Pallas kernels: none -> 53.7 us  [per_device(): pl.pallas_call(functools.partial(kernel, nd, ne), out_shape=jax.ShapeDtyp...]
    all_gather x1 -> x0, waiting for transfers between devices: 40.7 us -> none  [per_device(): lax.all_gather(arrived, 'dp', axis=1, tiled=True)]
    dot_general x3 -> x0, matrix products: 16.6 us -> none  [the longest x1 9.57 us: expert_ffn(): jnp.einsum('erf,efd->erd', hidden, w_down, preferred_element_type=jnp.flo...]
    all_to_all x1 -> x0, blocking collectives: 8.67 us -> none  [per_device(): lax.all_to_all(sel_rows, 'expert', split_axis=0, concat_axis=1, tiled=True)]
    all_to_all x1 -> x0, waiting for transfers between devices: 4.4 us -> none  [per_device(): lax.all_to_all(summed.astype(jnp.bfloat16), 'expert', split_axis=1, conca...]
    all_to_all x1 -> x0, starting transfers between devices: 3.33 us -> none  [per_device(): lax.all_to_all(summed.astype(jnp.bfloat16), 'expert', split_axis=1, conca...]
  transfers between devices with their start and end apart: 3 -> 0, of which waited for: 3 -> 0; matrix products, arithmetic and copies ran while one was open for 0% -> 0% of each run, Pallas kernels for 0% -> 0%
where the time goes in v1:
time: 56.1 us; the launch traced here: 56 us
  Pallas kernels  53.7 us (96%)
  local copies, waits for them, and re-layouts  2.29 us (4%)
    pallas_call x1, Pallas kernels, per_device(): pl.pallas_call(functools.partial(kernel, nd, ne), out_shape=jax.ShapeDtyp...  53.7 us
    unnamed x1, local copies, waits for them, and re-layouts  2.29 us

profile of v1, /device:TPU:0, one launch (start us, length us, event | category | flops | bytes accessed | tf_op | source)
XLA Modules:
  0.0 56.0 jit_solution(11186576005879770626)
XLA Ops:
  0.0 53.7 %shard_map.64 = bf16[128,4096]{1,0:T(8,128)(2,1)} custom-call(bf16[128,4096]{1,0:T(8,128)(2,1)} %tok.1, s32[4,4]{1,0:T(4,128)} %sel.1, f32[4,4]{1,0:T(4,128)} %gat.1, bf16[1,4096,1024]{2,1,0:T(8,128)(2,1)} %wg_hbm.1, bf16[1,4096,1024]{2,1,0:T(8,128)(2,1)} %wu_hbm.1, bf16[1,1024,4096]{2,1,0:T(8,128)(2,1)} %wd_hbm.1), custom_call_target="tpu_custom_call" | custom-call | tf_op jit(solution)/shard_map/pallas_call | solution.py:255
  53.7 2.3 %copy.8 = bf16[128,4096]{1,0:T(8,128)(2,1)} copy(bf16[128,4096]{1,0:T(8,128)(2,1)} %shard_map.64) | data formatting | bytes 2097152

commit v2 on v1

v2 whole, which is shorter than its diff:
```python
import functools

import jax
import jax.numpy as jnp
from jax import lax
from jax.experimental import pallas as pl
from jax.experimental.pallas import tpu as pltpu
from jax.sharding import PartitionSpec as P

MESH = pl.DeviceIdType.MESH
TILE = 16
F32 = jnp.float32
BF16 = jnp.bfloat16


def log2(n):
    return n.bit_length() - 1


def kernel(
    nd, ne, tok, sel, gat, wg_hbm, wu_hbm, wd_hbm, out,
    wg, wu, wd, sb, ab, x, g_acc, u_acc, hid, pb, xr, zb, zr, summed, rb, ob, cmb,
    w_sem, a_send, a_recv, gz_send, gz_recv, gx_send, gx_recv,
    rx_send, rx_recv, rz_send, rz_recv, o_send, o_recv,
):
    stages = x.shape[0]
    inner = x.shape[1]
    outer = x.shape[2]
    rows = x.shape[3]
    span = x.shape[4]
    slots = sel.shape[1]
    tokens_here = tok.shape[0]
    parts = TILE // slots
    wide = span // parts
    chunks = pb.shape[0]
    cols = pb.shape[4]
    dp = lax.axis_index("dp")
    ex = lax.axis_index("expert")
    za = dp // inner
    xb = lax.rem(dp, inner)
    other = (inner - 1) - xb

    def at_expert(d):
        return (dp, lax.rem(ex + d, ne))

    def at_outer(d):
        return (lax.rem(za + d, outer) * inner + xb, ex)

    partner = (za * inner + other, ex)

    def remote(src, dst, send, recv, to):
        return pltpu.make_async_remote_copy(
            src_ref=src, dst_ref=dst, send_sem=send, recv_sem=recv,
            device_id=to, device_id_type=MESH,
        )

    barrier = pltpu.get_barrier_semaphore()
    for d in range(1, ne):
        pl.semaphore_signal(barrier, inc=1, device_id=at_expert(d), device_id_type=MESH)
    for d in range(1, outer):
        pl.semaphore_signal(barrier, inc=1, device_id=at_outer(d), device_id_type=MESH)
    if inner > 1:
        pl.semaphore_signal(barrier, inc=1, device_id=partner, device_id_type=MESH)

    loads = [
        pltpu.make_async_copy(h.at[0], v, w_sem.at[i])
        for i, (h, v) in enumerate(((wg_hbm, wg), (wu_hbm, wu), (wd_hbm, wd)))
    ]
    for load in loads:
        load.start()

    packed = ne * TILE
    r_id = lax.broadcasted_iota(jnp.int32, (packed, tokens_here), 0)
    t_id = lax.broadcasted_iota(jnp.int32, (packed, tokens_here), 1)
    r_slot = ((r_id >> log2(TILE)) << log2(slots)) + (r_id & (slots - 1))
    r_part = (r_id & (TILE - 1)) >> log2(slots)
    named = jnp.full((packed, tokens_here), -1, jnp.int32)
    for e in range(ne):
        for s in range(slots):
            named = jnp.where(r_slot == e * slots + s, sel[e, s], named)
    hit = jnp.where(named == t_id, 1.0, 0.0)
    pick = jnp.concatenate(
        [jnp.where(r_part == p, hit, 0.0).astype(BF16) for p in range(parts)], axis=1
    )
    for q in range(stages):
        stack = jnp.concatenate(
            [tok[:, q * span + p * wide:q * span + (p + 1) * wide] for p in range(parts)], axis=0
        )
        gathered = jnp.dot(pick, stack, preferred_element_type=F32).astype(BF16)
        sb[q] = gathered.reshape(ne, TILE, wide)
        ab[q, ex] = sb[q, ex]

    pl.semaphore_wait(barrier, (ne - 1) + (outer - 1) + (1 if inner > 1 else 0))

    sent = []

    def start(copy):
        copy.start()
        sent.append(copy)

    for q in range(stages):
        for d in range(1, ne):
            to = at_expert(d)
            start(remote(sb.at[q, to[1]], ab.at[q, ex], a_send.at[q, d], a_recv.at[q, d], to))

    def packing(shape, packed_dim):
        r = lax.broadcasted_iota(jnp.int32, shape, packed_dim)
        k = lax.broadcasted_iota(jnp.int32, shape, 1 - packed_dim)
        col = (
            ((r & (TILE - 1)) >> log2(slots)) * rows
            + ((r >> log2(TILE)) << log2(slots)) + (r & (slots - 1))
        )
        return jnp.where(k == col, 1.0, 0.0).astype(BF16)

    pack = packing((packed, parts * rows), 0)
    unpack = packing((parts * rows, packed), 1)

    def gx(q, owner_b, d):
        block = x.at[q, owner_b, lax.rem(za + outer - d, outer)]
        return remote(block, block, gx_send.at[q, d], gx_recv.at[q, d], partner)

    def gz(q, d, owner_a):
        block = x.at[q, xb, owner_a]
        return remote(block, block, gz_send.at[q, d], gz_recv.at[q, d], at_outer(d))

    order = sorted(range(1, outer), key=lambda d: (min(d, outer - d), d))
    for q in range(stages):
        for d in range(1, ne):
            src = lax.rem(ex + ne - d, ne)
            remote(
                sb.at[q, src], ab.at[q, src], a_send.at[q, d], a_recv.at[q, d], at_expert(d)
            ).wait_recv()
        mine = jnp.dot(
            unpack, ab[q].reshape(packed, wide), preferred_element_type=F32
        ).astype(BF16)
        for p in range(parts):
            x[q, xb, za, :, p * wide:(p + 1) * wide] = mine[p * rows:(p + 1) * rows]
        for d in order:
            start(gz(q, d, za))
        if inner > 1:
            start(gx(q, xb, 0))

    terms = 3
    c_id = lax.broadcasted_iota(jnp.int32, (tokens_here, terms * packed), 1)
    n_id = lax.broadcasted_iota(jnp.int32, (tokens_here, terms * packed), 0)
    c_row = c_id & (packed - 1)
    c_slot = ((c_row >> log2(TILE)) << log2(slots)) + (c_row & (slots - 1))
    weight = jnp.zeros((tokens_here, terms * packed), F32)
    for e in range(ne):
        for s in range(slots):
            weight = jnp.where((c_slot == e * slots + s) & (n_id == sel[e, s]), gat[e, s], weight)
    left = weight
    coef = jnp.zeros_like(weight)
    for i in range(terms):
        term = left.astype(BF16).astype(F32)
        coef = jnp.where((c_id >> log2(packed)) == i, term, coef)
        left = left - term
    c_part = (c_row & (TILE - 1)) >> log2(slots)
    for p in range(parts):
        cmb[p] = jnp.where(c_part == p, coef, 0.0).astype(BF16)

    total_rows = inner * outer * rows
    step = min(256, hid.shape[1])

    def arrive(q):
        for d in order:
            gz(q, d, lax.rem(za + outer - d, outer)).wait_recv()
            if inner > 1:
                start(gx(q, xb, d))

    def multiply(q):
        if inner > 1:
            for d in [0] + order:
                gx(q, other, d).wait_recv()
        if q == 0:
            loads[0].wait()
            loads[1].wait()

        @pl.loop(0, hid.shape[1] // step)
        def _(i):
            at = pl.ds(pl.multiple_of(i * step, step), step)
            block = x[q].reshape(total_rows, span)
            g = jnp.dot(block, wg[q * span:(q + 1) * span, at], preferred_element_type=F32)
            u = jnp.dot(block, wu[q * span:(q + 1) * span, at], preferred_element_type=F32)
            if q > 0:
                g = g + g_acc[:, at]
                u = u + u_acc[:, at]
            if q < stages - 1:
                g_acc[:, at] = g
                u_acc[:, at] = u
            else:
                hid[:, at] = (g / (1.0 + jnp.exp(-g)) * u).astype(BF16)

    for q in range(stages):
        arrive(q)
        if q > 0:
            multiply(q - 1)
    multiply(stages - 1)

    loads[2].wait()

    def rx(c):
        return remote(pb.at[c, other], xr.at[c], rx_send.at[c], rx_recv.at[c], partner)

    @pl.loop(0, chunks)
    def _(c):
        at = pl.ds(pl.multiple_of(c * cols, cols), cols)
        part = jnp.dot(hid[...], wd[:, at], preferred_element_type=F32)
        pb[c] = part.astype(BF16).reshape(inner, outer, rows, cols)
        if inner > 1:
            rx(c).start()

    def rz(c, d):
        to = lax.rem(za + d, outer)
        return remote(zb.at[c, to], zr.at[c, d - 1], rz_send.at[c, d], rz_recv.at[c, d], at_outer(d))

    def inner_sum(c):
        value = pb[c, xb].astype(F32)
        if inner > 1:
            rx(c).wait_recv()
            value = value + xr[c].astype(F32)
        zb[c] = value.astype(BF16)
        for d in order:
            rz(c, d).start()

    per = span // cols

    def outer_sum(c):
        value = zb[c, za].astype(F32)
        for d in order:
            rz(c, d).wait_recv()
            value = value + zr[c, d - 1].astype(F32)
        for k in range(cols // wide):
            p = (c % per) * (cols // wide) + k
            summed[c // per, p] = value[:, k * wide:(k + 1) * wide].astype(BF16)

    def give(q):
        back = jnp.dot(pack, summed[q].reshape(parts * rows, wide), preferred_element_type=F32)
        rb[q] = back.astype(BF16).reshape(ne, TILE, wide)
        ob[q, ex] = rb[q, ex]
        for d in range(1, ne):
            to = at_expert(d)
            start(remote(rb.at[q, to[1]], ob.at[q, ex], o_send.at[q, d], o_recv.at[q, d], to))

    def mix(q):
        for d in range(1, ne):
            src = lax.rem(ex + ne - d, ne)
            remote(
                rb.at[q, src], ob.at[q, src], o_send.at[q, d], o_recv.at[q, d], at_expert(d)
            ).wait_recv()
        got = ob[q].reshape(packed, wide)
        total = jnp.dot(
            cmb[...].reshape(parts * tokens_here, terms * packed),
            jnp.concatenate([got] * terms, axis=0),
            preferred_element_type=F32,
        ).astype(BF16)
        for p in range(parts):
            at = q * span + p * wide
            out[:, at:at + wide] = total[p * tokens_here:(p + 1) * tokens_here]

    lag = min(3, chunks)
    for c in range(chunks + lag):
        if c < chunks:
            inner_sum(c)
        done = c - lag
        if done >= 0:
            outer_sum(done)
            if done % per == per - 1:
                give(done // per)
                if done // per > 0:
                    mix(done // per - 1)
    mix(stages - 1)

    for copy in sent:
        copy.wait_send()

    @pl.loop(0, chunks)
    def _(c):
        if inner > 1:
            rx(c).wait_send()
        for d in range(1, outer):
            rz(c, d).wait_send()


def per_device(nd, ne, tokens, select, gates, w_gate, w_up, w_down):
    tok_dev, width = tokens.shape
    slots = select.shape[1]
    hidden = w_gate.shape[2]
    inner = 2 if nd % 2 == 0 else 1
    outer = nd // inner
    rows = ne * slots
    parts = TILE // slots
    stages = 4
    span = width // stages
    wide = span // parts
    cols = span // 2
    chunks = width // cols
    vmem = pl.BlockSpec(memory_space=pltpu.VMEM)
    smem = pl.BlockSpec(memory_space=pltpu.SMEM)
    hbm = pl.BlockSpec(memory_space=pl.ANY)
    dma = pltpu.SemaphoreType.DMA
    return pl.pallas_call(
        functools.partial(kernel, nd, ne),
        out_shape=jax.ShapeDtypeStruct((tok_dev, width), BF16),
        in_specs=[vmem, smem, smem, hbm, hbm, hbm],
        out_specs=vmem,
        scratch_shapes=[
            pltpu.VMEM((width, hidden), BF16),
            pltpu.VMEM((width, hidden), BF16),
            pltpu.VMEM((hidden, width), BF16),
            pltpu.VMEM((stages, ne, TILE, wide), BF16),
            pltpu.VMEM((stages, ne, TILE, wide), BF16),
            pltpu.VMEM((stages, inner, outer, rows, span), BF16),
            pltpu.VMEM((nd * rows, hidden), F32),
            pltpu.VMEM((nd * rows, hidden), F32),
            pltpu.VMEM((nd * rows, hidden), BF16),
            pltpu.VMEM((chunks, inner, outer, rows, cols), BF16),
            pltpu.VMEM((chunks, outer, rows, cols), BF16),
            pltpu.VMEM((chunks, outer, rows, cols), BF16),
            pltpu.VMEM((chunks, max(outer - 1, 1), rows, cols), BF16),
            pltpu.VMEM((stages, parts, rows, wide), BF16),
            pltpu.VMEM((stages, ne, TILE, wide), BF16),
            pltpu.VMEM((stages, ne, TILE, wide), BF16),
            pltpu.VMEM((parts, tok_dev, 3 * ne * TILE), BF16),
            dma((3,)),
            dma((stages, ne)), dma((stages, ne)),
            dma((stages, outer)), dma((stages, outer)),
            dma((stages, outer)), dma((stages, outer)),
            dma((chunks,)), dma((chunks,)),
            dma((chunks, outer)), dma((chunks, outer)),
            dma((stages, ne)), dma((stages, ne)),
        ],
        compiler_params=pltpu.CompilerParams(
            collective_id=0, has_side_effects=True, vmem_limit_bytes=60 * 1024 * 1024
        ),
    )(tokens, select, gates, w_gate, w_up, w_down)


def solution(mesh):
    return jax.shard_map(
        functools.partial(per_device, mesh.shape["dp"], mesh.shape["expert"]),
        mesh=mesh,
        in_specs=(
            P(("dp", "expert"), None),
            P(None, ("dp", "expert")),
            P(None, ("dp", "expert")),
            P("expert", None, "dp"),
            P("expert", None, "dp"),
            P("expert", "dp", None),
        ),
        out_specs=P(("dp", "expert"), None),
        check_vma=False,
    )
```

time: 56.1 us -> 54.9 us (0.979)
  Pallas kernels: 53.7 us -> 52.5 us
    pallas_call x1, Pallas kernels: 53.7 us -> 52.5 us  [per_device(): pl.pallas_call(functools.partial(kernel, nd, ne), out_shape=jax.ShapeDtyp...]
where the time goes in v2:
time: 54.9 us; the launch traced here: 54.8 us
  Pallas kernels  52.5 us (96%)
  local copies, waits for them, and re-layouts  2.29 us (4%)
    pallas_call x1, Pallas kernels, per_device(): pl.pallas_call(functools.partial(kernel, nd, ne), out_shape=jax.ShapeDtyp...  52.5 us
    unnamed x1, local copies, waits for them, and re-layouts  2.29 us

profile of v2, /device:TPU:0, one launch (start us, length us, event | category | flops | bytes accessed | tf_op | source)
XLA Modules:
  0.0 54.8 jit_solution(7306230156656343088)
XLA Ops:
  0.0 52.5 %shard_map.64 = bf16[128,4096]{1,0:T(8,128)(2,1)} custom-call(bf16[128,4096]{1,0:T(8,128)(2,1)} %tok.1, s32[4,4]{1,0:T(4,128)} %sel.1, f32[4,4]{1,0:T(4,128)} %gat.1, bf16[1,4096,1024]{2,1,0:T(8,128)(2,1)} %wg_hbm.1, bf16[1,4096,1024]{2,1,0:T(8,128)(2,1)} %wu_hbm.1, bf16[1,1024,4096]{2,1,0:T(8,128)(2,1)} %wd_hbm.1), custom_call_target="tpu_custom_call" | custom-call | tf_op jit(solution)/shard_map/pallas_call | solution.py:302
  52.5 2.3 %copy.8 = bf16[128,4096]{1,0:T(8,128)(2,1)} copy(bf16[128,4096]{1,0:T(8,128)(2,1)} %shard_map.64) | data formatting | bytes 2097152
